TPU v7x, 256 devices: a whole 4x4x8 slice. The times are simulated.
256 devices in a mesh: epoch: 16 (over y, x), blend: 16 (over z, core).
Axes of the slice: x: 4, y: 4, z: 8, core: 2. Of those that a mesh axis runs over, the one named last changes fastest.
Arguments:
- visit_flux: bfloat16 [64, 64, 6, 16384], P('epoch', None, None, 'blend'), may hold values from -6 to 6
- visit_precision: bfloat16 [64, 64, 6, 16384], P('epoch', None, None, 'blend'), may hold values from 0.25 to 4
- visit_live: int32 [64, 64], P('epoch'), may hold values 0 or 1
- footprint: int32 [64, 8, 16384], P('blend', None, 'epoch'), may hold values 0 or 1
- source_count: int32 [64], P('blend'), may hold values from 1 to 8
- spectra_init: float32 [64, 8, 6], P('blend'), may hold values from 0.2 to 1.2
- morphology_init: float32 [64, 8, 16384], P('blend', None, 'epoch'), may hold values from 0 to 0.25
Outputs:
- coadd_flux: float32 [64, 6, 16384], P('blend', None, 'epoch')
- spectra: float32 [64, 8, 6], P('blend')
- morphology: float32 [64, 8, 16384], P('blend', None, 'epoch')
All inputs are finite; a program needn't handle non-finite values. No bound on the sum of `visit_live` or of `footprint` on one device may be relied on, other than what follows from the above.
Results may differ from a plain program's by a relative error of at most 0.0003.
Values sent between devices are 32-bit elements; how exact they have to be, the bound alone decides.
No kernel may reach another device: no remote copies, remote signals or barrier semaphores. Data moves between devices by JAX's collectives and lax.ppermute only.
A program may use at most 64 MiB of HBM per device.

v0:
```python
import jax
import jax.numpy as jnp
from jax import lax
from jax.experimental import pallas as pl
from jax.experimental.pallas import tpu as pltpu
from jax.sharding import PartitionSpec as P


VISIT_VMEM = 52 * 2**20
F32 = jnp.float32
VMEM = pl.BlockSpec(memory_space=pltpu.VMEM)
ANY = pl.BlockSpec(memory_space=pl.ANY)


def held_group(e, i):
    return 2 * ((e // 2 + 4 * (i % 2) - i // 2) % 8) + (e + i) % 2


def visit_kernel(first, flux_ref, prec_ref, live_ref, *rest):
    if first:
        outs, (live_out, flux_buf, prec_buf, live_buf, square, sems, live_sem) = rest[:8], rest[8:]
    else:
        outs, (flux_buf, prec_buf, sems) = rest[:8], rest[8:]
    e, i = lax.axis_index("epoch"), lax.axis_index("blend")
    odd = lax.rem(e + i, 2) == 1
    bands, visits, tiles = flux_buf.shape[:3]
    width = flux_buf.shape[4]
    base = 0 if first else bands
    copies = []
    if first:
        live_copy = pltpu.make_async_copy(live_ref, live_buf, live_sem)
        live_copy.start()
    for c in range(bands):
        row = []
        for v in range(visits):
            row.append(pltpu.make_async_copy(prec_ref.at[v, base + c], prec_buf.at[c, v], sems.at[0, c, v]))
            row.append(pltpu.make_async_copy(flux_ref.at[v, base + c], flux_buf.at[c, v], sems.at[1, c, v]))
        for copy in row:
            copy.start()
        copies.append(row)
    if first:
        live_copy.wait()
        square[...] = jnp.zeros(square.shape, F32)
        square[:visits, : 8 * tiles] = live_buf[...].astype(F32)
        turned = jnp.transpose(square[...])
        for v in range(visits):
            live_out[v] = jnp.broadcast_to(turned[: 8 * tiles, v : v + 1], (8 * tiles, 128)).reshape(tiles, 8, 128)
        live = live_out
    else:
        live = live_ref
    low_rows = lax.broadcasted_iota(jnp.int32, (8, 128), 0) < 4
    for c in range(bands):
        for copy in copies[c]:
            copy.wait()
        for j in range(tiles):
            pair = lax.rem(lax.bitwise_xor(lax.div(e, 2), j) + 4 * lax.rem(i, 2) + 8 - lax.div(i, 2), 8)
            lives = [live[v, pair] for v in range(visits)]
            x, y = 2 * (j % 2), j // 2
            (far0, far1), (at0, at1) = ((x, x + 1), (y, y)) if first else ((y, y), (x, x + 1))
            even, uneven = outs[2 * far0 + at0 // 2].at[at0 % 2], outs[2 * far1 + at1 // 2].at[at1 % 2]

            def lane_tile(l, _, c=c, pair=pair, lives=lives, even=even, uneven=uneven):
                lanes = pl.ds(pl.multiple_of(l * 128, 128), 128)
                num = wsum = None
                for v in range(visits):
                    w = prec_buf[c, v, pair, :, lanes].astype(F32) * lives[v]
                    n = w * flux_buf[c, v, pair, :, lanes].astype(F32)
                    num, wsum = (n, w) if v == 0 else (num + n, wsum + w)
                low = jnp.where(low_rows, num, pltpu.roll(wsum, 4, 0))
                high = jnp.where(low_rows, pltpu.roll(num, 4, 0), wsum)
                even[c, :, lanes] = jnp.where(odd, high, low)
                uneven[c, :, lanes] = jnp.where(odd, low, high)
                return 0

            lax.fori_loop(0, width // 128, lane_tile, 0, unroll=True)


def visit_sums(first, flux, prec, live):
    visits, bands, tiles, _, width = flux.shape
    half = bands // 2
    piece = jax.ShapeDtypeStruct((2, half, 8, width), F32)
    buf = pltpu.VMEM((half, visits, tiles, 8, width), flux.dtype)
    work = visits * half * tiles * 8 * width
    outs, scratch = [piece] * 8, [buf, buf, pltpu.SemaphoreType.DMA((2, half, visits))]
    if first:
        outs.append(jax.ShapeDtypeStruct((visits, tiles, 8, 128), F32))
        scratch[2:2] = [pltpu.VMEM(live.shape, live.dtype), pltpu.VMEM((128, 128), F32)]
        scratch.append(pltpu.SemaphoreType.DMA)
    return pl.pallas_call(
        lambda *refs: visit_kernel(first, *refs),
        out_shape=outs,
        in_specs=[ANY, ANY, ANY if first else VMEM],
        out_specs=[VMEM] * len(outs),
        scratch_shapes=scratch,
        compiler_params=pltpu.CompilerParams(vmem_limit_bytes=VISIT_VMEM),
        cost_estimate=pl.CostEstimate(flops=8 * work, bytes_accessed=4 * work, transcendentals=0),
        name="visit_first" if first else "visit_second",
    )(flux, prec, live)


def pass_kernel(a, b, c, d, low, high):
    low[...] = a[...] + b[...]
    high[...] = c[...] + d[...]


def pass_all_kernel(near0, mid0, far1, mid1, far0, near1, low, high):
    low[:2] = near0[...]
    low[2:] = mid0[...] + far1[...]
    high[:2] = mid1[...] + far0[...]
    high[2:] = near1[...]


def join_all_kernel(own0, own1, low, high, *outs):
    for n, out in enumerate(outs):
        out[...] = (own0, own1)[n // 2][n % 2] + low[n] + high[n]


def join_kernel(*refs):
    ins, outs = refs[:6], refs[6:]
    for n, out in enumerate(outs):
        a, b, c = ins[3 * (n // 2) : 3 * (n // 2) + 3]
        out[...] = a[n % 2] + b[n % 2] + c[n % 2]


def spread(tile, n):
    return jnp.broadcast_to(tile[:, n : n + 1], tile.shape)


def step_body(s, many, coadd_ref, cover_ref, morph, mask_ref, morph_out, resid_ref, payload_ref):
    halves, width = resid_ref.shape[0], resid_ref.shape[2]
    slots = mask_ref.shape[0]
    sb = [[spread(s, cc * slots + k) for cc in range(halves)] for k in range(slots)]
    steps = []
    for k in range(slots):
        sq = sb[k][0] * sb[k][0]
        for cc in range(1, halves):
            sq = sq + sb[k][cc] * sb[k][cc]
        sq = sq + pltpu.roll(sq, 4, 0)
        steps.append(1.0 / (1.0 + many * sq))

    def residual(ms, cc, lanes):
        model = sb[0][cc] * ms[0]
        for k in range(1, slots):
            model = model + sb[k][cc] * ms[k]
        return cover_ref[cc, :, lanes] * (coadd_ref[cc, :, lanes] - model)

    def lane_tile(l, _):
        lanes = pl.ds(pl.multiple_of(l * 128, 128), 128)
        ms = [morph[k, :, lanes] for k in range(slots)]
        rs = [residual(ms, cc, lanes) for cc in range(halves)]
        new = []
        for k in range(slots):
            grad = sb[k][0] * rs[0]
            for cc in range(1, halves):
                grad = grad + sb[k][cc] * rs[cc]
            grad = grad + pltpu.roll(grad, 4, 0)
            m = jnp.maximum(0.0, ms[k] + grad * steps[k]) * mask_ref[k, :, lanes]
            morph_out[k, :, lanes] = m
            new.append(m)
        for cc in range(halves):
            resid_ref[cc, :, lanes] = residual(new, cc, lanes)
        return 0

    lax.fori_loop(0, width // 128, lane_tile, 0, unroll=True)
    lane = lax.broadcasted_iota(jnp.int32, (8, 128), 1)
    total = jnp.zeros((8, 128), F32)
    rs = [resid_ref[cc] for cc in range(halves)]
    for k in range(slots):
        m = morph_out[k]
        for cc in range(halves):
            got = jnp.sum(m * rs[cc], axis=1, keepdims=True)
            total = jnp.where(lane == cc * slots + k, got, total)
        got = jnp.sum(m * m, axis=1, keepdims=True)
        total = jnp.where(lane == halves * slots + k, got, total)
    for n in range(payload_ref.shape[0]):
        payload_ref[n] = total


def spectra_step(s, many, arrived_ref, halves, slots):
    total = arrived_ref[0]
    for n in range(1, arrived_ref.shape[0]):
        total = total + arrived_ref[n]
    lane = lax.broadcasted_iota(jnp.int32, (8, 128), 1)
    norm = total
    for cc in range(halves):
        moved = pltpu.roll(total, 128 - (halves - cc) * slots, 1)
        norm = jnp.where((lane >= cc * slots) & (lane < (cc + 1) * slots), moved, norm)
    new = jnp.maximum(0.0, s + total / (1.0 + many * norm))
    return jnp.where(lane < halves * slots, new, 0.0)


def total_kernel(*refs):
    out = refs[8]
    half = out.shape[0] // 2
    for n in range(2):
        a, b, c, d = refs[4 * n : 4 * n + 4]
        out[n * half : (n + 1) * half] = (a[...] + b[...]) + (c[...] + d[...])


def first_kernel(
    sums_ref, mask_ref, morph_ref, s_ref, many_ref, coadd_ref, cover_ref, morph_out, payload_ref, resid_ref
):
    halves, width = coadd_ref.shape[0], coadd_ref.shape[2]
    low_rows = lax.broadcasted_iota(jnp.int32, (8, 128), 0) < 4

    def lane_tile(l, _):
        lanes = pl.ds(pl.multiple_of(l * 128, 128), 128)
        got = [sums_ref[n, :, lanes] for n in range(2 * halves)]
        for cc in range(halves):
            even, uneven = got[2 * cc], got[2 * cc + 1]
            num = jnp.where(low_rows, even, pltpu.roll(uneven, 4, 0))
            wsum = jnp.where(low_rows, pltpu.roll(even, 4, 0), uneven)
            below = 1.0 / (1.0 + wsum)
            coadd_ref[cc, :, lanes] = num * below
            cover_ref[cc, :, lanes] = wsum * below
        return 0

    lax.fori_loop(0, width // 128, lane_tile, 0, unroll=True)
    step_body(s_ref[...], many_ref[...], coadd_ref, cover_ref, morph_ref, mask_ref, morph_out, resid_ref, payload_ref)


def next_kernel(arrived_ref, s_ref, many_ref, coadd_ref, cover_ref, morph_ref, mask_ref, s_out, morph_out, payload_ref, resid_ref):
    halves, slots = coadd_ref.shape[0], mask_ref.shape[0]
    s = spectra_step(s_ref[...], many_ref[...], arrived_ref, halves, slots)
    s_out[...] = s
    step_body(s, many_ref[...], coadd_ref, cover_ref, morph_ref, mask_ref, morph_out, resid_ref, payload_ref)


def last_kernel(arrived_ref, s_ref, many_ref, out_ref):
    bands, owned, slots = out_ref.shape
    s = spectra_step(s_ref[...], many_ref[...], arrived_ref, bands // 2, slots)
    for c in range(bands):
        out_ref[c] = s[(c % 2) * owned : (c % 2 + 1) * owned, (c // 2) * slots : (c // 2 + 1) * slots]


def call(kernel, outs, args, scratch=()):
    return pl.pallas_call(
        kernel,
        out_shape=[jax.ShapeDtypeStruct(o, F32) for o in outs],
        in_specs=[VMEM] * len(args),
        out_specs=[VMEM] * len(outs),
        scratch_shapes=[pltpu.VMEM(s, F32) for s in scratch],
        compiler_params=pltpu.CompilerParams(vmem_limit_bytes=8 * 2**20),
        cost_estimate=pl.CostEstimate(flops=4_000_000, bytes_accessed=1_000_000, transcendentals=0),
    )(*args)


def on_device(visit_flux, visit_precision, visit_live, footprint, source_count, spectra_init, morphology_init):
    n_epoch, n_blend = lax.axis_size("epoch"), lax.axis_size("blend")
    owned, slots, width = footprint.shape
    bands = visit_flux.shape[2]
    halves = bands // 2

    def hop(a, m):
        return lax.ppermute(a, "epoch", [(e, e ^ m) for e in range(n_epoch)])


    tiled = lambda a: jnp.transpose(a, (0, 2, 1, 3)).reshape(a.shape[0], bands, a.shape[1] // 8, 8, a.shape[3])
    flux, prec = tiled(visit_flux), tiled(visit_precision)
    both_ways = lambda a, b, step: (hop(a, step), hop(b, 3 * step))
    *a, live = visit_sums(True, flux, prec, visit_live)
    b = visit_sums(False, flux, prec, live)
    a_far = both_ways(a[4], a[5], 1)
    b_far = both_ways(b[4], b[5], 4)
    b_near = both_ways(b[2], b[7], 4)
    two = (2, halves, 8, width)
    four = (4, halves, 8, width)
    a_last = both_ways(*call(pass_all_kernel, [four] * 2, [a[2], a[3], a_far[1], a[6], a_far[0], a[7]], ()), 1)
    b_last = both_ways(*call(pass_kernel, [two] * 2, [b[3], b_far[1], b[6], b_far[0]], ()), 4)

    piece = (halves, 8, width)
    home = [(e * n_blend + i, i * n_blend + held_group(e, i)) for e in range(n_epoch) for i in range(n_blend)]
    a = call(join_all_kernel, [piece] * 4, [a[0], a[1], *a_last], ())
    a = [a[0]] + [hop(a[m], 4 * m) for m in (2, 1, 3)]
    b = call(join_kernel, [piece] * 4, [b[0], b_near[0], b_last[1], b[1], b_near[1], b_last[0]], ())
    b = [b[0]] + [hop(b[m], m) for m in (2, 1, 3)]
    (total,) = call(total_kernel, [(bands, 8, width)], [*a, *b], ())
    sums = lax.ppermute(total, ("epoch", "blend"), home)

    source_live = (jnp.arange(slots, dtype=jnp.int32)[None, :] < source_count[:, None]).astype(F32)
    mask = footprint.astype(F32) * source_live[:, :, None]
    twice = lambda a: jnp.concatenate([a, a], axis=1)
    mask_t = twice(jnp.transpose(mask, (1, 0, 2)))
    morph_t = twice(jnp.transpose(morphology_init * mask, (1, 0, 2)))
    many = jnp.broadcast_to(jnp.tile(source_count.astype(F32), 2)[:, None], (8, 128))
    s = jnp.transpose(spectra_init.reshape(owned, slots, halves, 2), (3, 0, 2, 1)).reshape(2 * owned, halves * slots)
    s = jnp.pad(s, ((0, 0), (0, 128 - halves * slots)))

    tile3, tile8 = (halves, 8, width), (slots, 8, width)
    payload = (n_epoch, 8, 128)
    coadd, cover, morph, sent = call(
        first_kernel, [tile3, tile3, tile8, payload], [sums, mask_t, morph_t, s, many], [tile3]
    )
    swap_all = lambda a: lax.all_to_all(a, "epoch", split_axis=0, concat_axis=0, tiled=True)
    s, morph, sent = call(
        next_kernel, [(8, 128), tile8, payload], [swap_all(sent), s, many, coadd, cover, morph, mask_t], [tile3]
    )
    (spectra,) = call(last_kernel, [(bands, owned, slots)], [swap_all(sent), s, many], ())
    coadd = jnp.transpose(coadd.reshape(bands, owned, width), (1, 0, 2))
    return coadd, jnp.transpose(spectra, (1, 2, 0)), jnp.transpose(morph[:, :owned], (1, 0, 2))


def solution(mesh):
    in_specs = (
        P("epoch", None, None, "blend"),
        P("epoch", None, None, "blend"),
        P("epoch", None),
        P("blend", None, "epoch"),
        P("blend"),
        P("blend", None, None),
        P("blend", None, "epoch"),
    )
    out_specs = (P("blend", None, "epoch"), P("blend", None, None), P("blend", None, "epoch"))
    return jax.shard_map(on_device, mesh=mesh, in_specs=in_specs, out_specs=out_specs, check_vma=False)
```

profile of v0, /device:TPU:2, one launch (start us, length us, event | category | flops | bytes accessed | tf_op | source)
XLA Modules:
  0.0 82.5 jit_solution(1649685760773745056)
XLA Ops:
  0.6 0.0 copy-start
  0.6 0.7 copy-done
  1.3 2.4 %visit_first.1 = (f32[2,3,8,1024]{3,2,1,0:T(8,128)S(1)}, f32[2,3,8,1024]{3,2,1,0:T(8,128)S(1)}, f32[2,3,8,1024]{3,2,1,0:T(8,128)S(1)}, f32[2,3,8,1024]{3,2,1,0:T...) custom-call(bf16[4,6,8,8,1024]{4,3,2,1,0:T(8,128)(2,1)} %bitcast.18,, ...), custom_call_target="tpu_custom_call" | custom-call | flops 6291456 | bytes 3145728 | tf_op jit(solution)/shard_map/visit_first/pallas_call | solution.py:89
  3.7 1.6 %collective-permute-start = (f32[2,3,8,1024]{3,2,1,0:T(8,128)S(1)}, f32[2,3,8,1024]{3,2,1,0:T(8,128)S(1)}, u32[]{:S(2)}, u32[]{:S(2)}) collective-permute-start(f32[2,3,8,1024]{3,2,1,0:T(8,128)S(1)} %get-tuple-element.43), channel_id=1, source_target_pairs={{0,48},{16,32},{32,16},{48,0},{64,112},{80,96},{96,80},{112,64},{1... | collective-permute-start | bytes 589832 | tf_op jit(solution)/shard_map/ppermute | solution.py:255
  5.3 1.8 %collective-permute-start.1 = (f32[2,3,8,1024]{3,2,1,0:T(8,128)S(1)}, f32[2,3,8,1024]{3,2,1,0:T(8,128)S(1)}, u32[]{:S(2)}, u32[]{:S(2)}) collective-permute-start(f32[2,3,8,1024]{3,2,1,0:T(8,128)S(1)} %get-tuple-element.45), channel_id=1, source_target_pairs={{0,16},{16,0},{32,48},{48,32},{64,80},{80,64},{96,112},{112,96},{1... | collective-permute-start | bytes 589832 | tf_op jit(solution)/shard_map/ppermute | solution.py:255
  7.1 2.4 %visit_second.1 = (f32[2,3,8,1024]{3,2,1,0:T(8,128)S(1)}, f32[2,3,8,1024]{3,2,1,0:T(8,128)S(1)}, f32[2,3,8,1024]{3,2,1,0:T(8,128)S(1)}, f32[2,3,8,1024]{3,2,1,0:...) custom-call(bf16[4,6,8,8,1024]{4,3,2,1,0:T(8,128)(2,1)} %bitcast.19,, ...), custom_call_target="tpu_custom_call" | custom-call | flops 6291456 | bytes 3145728 | tf_op jit(solution)/shard_map/visit_second/pallas_call | solution.py:89
  9.4 0.0 copy-start.4
  9.5 0.0 copy-start.1
  9.5 0.0 copy-start.2
  9.5 0.0 copy-start.3
  9.5 3.1 %collective-permute-start.8 = (f32[2,3,8,1024]{3,2,1,0:T(8,128)S(1)}, f32[2,3,8,1024]{3,2,1,0:T(8,128)S(1)}, u32[]{:S(2)}, u32[]{:S(2)}) collective-permute-start(f32[2,3,8,1024]{3,2,1,0:T(8,128)S(1)} %get-tuple-element.57), channel_id=1, source_target_pairs={{0,192},{16,208},{32,224},{48,240},{64,128},{80,144},{96,160},{112... | collective-permute-start | bytes 589832 | tf_op jit(solution)/shard_map/ppermute | solution.py:255
  12.6 0.1 collective-permute-start.9
  12.7 1.9 %collective-permute-start.7 = (f32[2,3,8,1024]{3,2,1,0:T(8,128)S(1)}, f32[2,3,8,1024]{3,2,1,0:T(8,128)S(1)}, u32[]{:S(2)}, u32[]{:S(2)}) collective-permute-start(f32[2,3,8,1024]{3,2,1,0:T(8,128)S(1)} %get-tuple-element.55), channel_id=1, source_target_pairs={{0,64},{16,80},{32,96},{48,112},{64,0},{80,16},{96,32},{112,48},{1... | collective-permute-start | bytes 589832 | tf_op jit(solution)/shard_map/ppermute | solution.py:255
  14.6 0.0 collective-permute-done.far1
  14.6 0.0 collective-permute-done.1.far0
  14.6 0.1 shard_map.94
  14.7 0.3 collective-permute-start.2
  15.0 0.5 collective-permute-start.3
  15.5 1.4 %collective-permute-done.8.b = f32[2,3,8,1024]{3,2,1,0:T(8,128)S(1)} collective-permute-done((f32[2,3,8,1024]{3,2,1,0:T(8,128)S(1)}, f32[2,3,8,1024]{3,2,1,0:T(8,128)S(1)}, u32[]{:S(2)}, u32[]{:S(2)}) %collective-permute-start.8) | collective-permute-done | bytes 196640 | tf_op jit(solution)/shard_map/ppermute | solution.py:255
  16.9 3.0 %collective-permute-start.11 = (f32[2,3,8,1024]{3,2,1,0:T(8,128)S(1)}, f32[2,3,8,1024]{3,2,1,0:T(8,128)S(1)}, u32[]{:S(2)}, u32[]{:S(2)}) collective-permute-start(f32[2,3,8,1024]{3,2,1,0:T(8,128)S(1)} %get-tuple-element.62), channel_id=1, source_target_pairs={{0,192},{16,208},{32,224},{48,240},{64,128},{80,144},{96,160},{112... | collective-permute-start | bytes 589832 | tf_op jit(solution)/shard_map/ppermute | solution.py:255
  19.9 0.5 collective-permute-done.9.d
  20.4 0.3 collective-permute-start.10
  20.7 1.9 %collective-permute-done.7.refs_1_ = f32[2,3,8,1024]{3,2,1,0:T(8,128)S(1)} collective-permute-done((f32[2,3,8,1024]{3,2,1,0:T(8,128)S(1)}, f32[2,3,8,1024]{3,2,1,0:T(8,128)S(1)}, u32[]{:S(2)}, u32[]{:S(2)}) %collective-permute-start.7) | collective-permute-done | bytes 196640 | tf_op jit(solution)/shard_map/ppermute | solution.py:255
  22.6 0.3 collective-permute-start.12
  22.9 2.8 %collective-permute-done.11.refs_4_ = f32[2,3,8,1024]{3,2,1,0:T(8,128)S(1)} collective-permute-done((f32[2,3,8,1024]{3,2,1,0:T(8,128)S(1)}, f32[2,3,8,1024]{3,2,1,0:T(8,128)S(1)}, u32[]{:S(2)}, u32[]{:S(2)}) %collective-permute-start.11) | collective-permute-done | bytes 196640 | tf_op jit(solution)/shard_map/ppermute | solution.py:255
  25.7 2.4 %collective-permute-done.10.refs_2_ = f32[2,3,8,1024]{3,2,1,0:T(8,128)S(1)} collective-permute-done((f32[2,3,8,1024]{3,2,1,0:T(8,128)S(1)}, f32[2,3,8,1024]{3,2,1,0:T(8,128)S(1)}, u32[]{:S(2)}, u32[]{:S(2)}) %collective-permute-start.10) | collective-permute-done | bytes 196640 | tf_op jit(solution)/shard_map/ppermute | solution.py:255
  28.0 0.2 collective-permute-done.12.refs_5_
  28.3 0.1 shard_map.97
  28.3 0.8 collective-permute-start.13
  29.1 1.2 %collective-permute-start.14 = (f32[3,8,1024]{2,1,0:T(8,128)S(1)}, f32[3,8,1024]{2,1,0:T(8,128)S(1)}, u32[]{:S(2)}, u32[]{:S(2)}) collective-permute-start(f32[3,8,1024]{2,1,0:T(8,128)S(1)} %get-tuple-element.66), channel_id=1, source_target_pairs={{0,16},{16,0},{32,48},{48,32},{64,80},{80,64},{96,112},{112,96},{1... | collective-permute-start | bytes 294920 | tf_op jit(solution)/shard_map/ppermute | solution.py:255
  30.4 2.1 %collective-permute-start.15 = (f32[3,8,1024]{2,1,0:T(8,128)S(1)}, f32[3,8,1024]{2,1,0:T(8,128)S(1)}, u32[]{:S(2)}, u32[]{:S(2)}) collective-permute-start(f32[3,8,1024]{2,1,0:T(8,128)S(1)} %get-tuple-element.67), channel_id=1, source_target_pairs={{0,48},{16,32},{32,16},{48,0},{64,112},{80,96},{96,80},{112,64},{1... | collective-permute-start | bytes 294920 | tf_op jit(solution)/shard_map/ppermute | solution.py:255
  32.5 0.0 collective-permute-done.2.low
  32.5 0.0 collective-permute-done.3.high
  32.5 0.1 shard_map.95
  32.6 0.7 collective-permute-start.4
  33.3 2.5 %collective-permute-start.5 = (f32[3,8,1024]{2,1,0:T(8,128)S(1)}, f32[3,8,1024]{2,1,0:T(8,128)S(1)}, u32[]{:S(2)}, u32[]{:S(2)}) collective-permute-start(f32[3,8,1024]{2,1,0:T(8,128)S(1)} %get-tuple-element.51), channel_id=1, source_target_pairs={{0,64},{16,80},{32,96},{48,112},{64,0},{80,16},{96,32},{112,48},{1... | collective-permute-start | bytes 294920 | tf_op jit(solution)/shard_map/ppermute | solution.py:255
  35.8 0.0 collective-permute-done.13.refs_5_
  35.8 1.1 %collective-permute-start.6 = (f32[3,8,1024]{2,1,0:T(8,128)S(1)}, f32[3,8,1024]{2,1,0:T(8,128)S(1)}, u32[]{:S(2)}, u32[]{:S(2)}) collective-permute-start(f32[3,8,1024]{2,1,0:T(8,128)S(1)} %get-tuple-element.52), channel_id=1, source_target_pairs={{0,192},{16,208},{32,224},{48,240},{64,128},{80,144},{96,160},{112... | collective-permute-start | bytes 294920 | tf_op jit(solution)/shard_map/ppermute | solution.py:255
  36.9 0.0 copy-done.4
  36.9 0.0 collective-permute-done.14.refs_6_
  36.9 0.0 collective-permute-done.15.refs_7_
  36.9 1.9 %collective-permute-done.4.refs_1_ = f32[3,8,1024]{2,1,0:T(8,128)S(1)} collective-permute-done((f32[3,8,1024]{2,1,0:T(8,128)S(1)}, f32[3,8,1024]{2,1,0:T(8,128)S(1)}, u32[]{:S(2)}, u32[]{:S(2)}) %collective-permute-start.4) | collective-permute-done | bytes 98336 | tf_op jit(solution)/shard_map/ppermute | solution.py:255
  38.8 0.6 collective-permute-done.5.refs_2_
  39.4 2.2 %collective-permute-done.6.refs_3_ = f32[3,8,1024]{2,1,0:T(8,128)S(1)} collective-permute-done((f32[3,8,1024]{2,1,0:T(8,128)S(1)}, f32[3,8,1024]{2,1,0:T(8,128)S(1)}, u32[]{:S(2)}, u32[]{:S(2)}) %collective-permute-start.6) | collective-permute-done | bytes 98336 | tf_op jit(solution)/shard_map/ppermute | solution.py:255
  41.7 1.9 %collective-permute-start.16 = (f32[6,8,1024]{2,1,0:T(8,128)S(1)}, f32[6,8,1024]{2,1,0:T(8,128)S(1)}, u32[]{:S(2)}, u32[]{:S(2)}) collective-permute-start(f32[6,8,1024]{2,1,0:T(8,128)S(1)} %shard_map.98), channel_id=1, source_target_pairs={{0,0},{1,25},{2,46},{3,55},{4,76},{5,85},{6,106},{7,115},{8,136},{... | collective-permute-start | bytes 589832 | tf_op jit(solution)/shard_map/ppermute | solution.py:278
  43.6 0.0 copy-done.1
  43.6 0.0 copy-done.2
  43.6 0.2 fusion
  43.8 0.0 copy-done.3
  43.8 0.1 reshape.48
  43.9 0.1 broadcast_in_dim.4
  44.0 0.1 pad_maximum_fusion
  44.1 6.1 %collective-permute-done.16.sums_ref = f32[6,8,1024]{2,1,0:T(8,128)S(1)} collective-permute-done((f32[6,8,1024]{2,1,0:T(8,128)S(1)}, f32[6,8,1024]{2,1,0:T(8,128)S(1)}, u32[]{:S(2)}, u32[]{:S(2)}) %collective-permute-start.16) | collective-permute-done | bytes 196640 | tf_op jit(solution)/shard_map/ppermute | solution.py:278
  50.2 0.1 broadcast_in_dim.5.many_ref
  50.2 1.1 %shard_map.99 = (f32[3,8,1024]{2,1,0:T(8,128)S(1)}, f32[3,8,1024]{2,1,0:T(8,128)S(1)}, f32[8,8,1024]{2,1,0:T(8,128)S(1)}, f32[16,8,128]{2,1,0:T(8,128)}) custom-call(f32[6,8,1024]{2,1,0:T(8,128)S(1)} %collective-permute-done.16.sums_ref, f32[8,8,1024]{2,1,0:T(8,128)S(1)} %get-tuple-element.83.mask_ref, f32[8,8,1024]{2,1,0:T(8,128)S(1)} %get-tuple-element.84.morph_ref, ...), custom_call_target="tpu_custom_call" | custom-call | flops 4000000 | bytes 1000000 | tf_op jit(solution)/shard_map/pallas_call | solution.py:237
  51.3 11.9 %all-to-all-start = ((f32[16,8,128]{2,1,0:T(8,128)}), f32[16,8,128]{2,1,0:T(8,128)S(1)}, u32[]{:S(2)}, u32[]{:S(2)}) async-start(f32[16,8,128]{2,1,0:T(8,128)} %get-tuple-element.69), calls=%async_computation | async-start | bytes 131072 | tf_op jit(solution)/shard_map/all_to_all | solution.py:294
  63.2 0.7 reshape.49
  63.9 5.6 %all-to-all-done.arrived_ref = f32[16,8,128]{2,1,0:T(8,128)S(1)} async-done(((f32[16,8,128]{2,1,0:T(8,128)}), f32[16,8,128]{2,1,0:T(8,128)S(1)}, u32[]{:S(2)}, u32[]{:S(2)}) %all-to-all-start) | async-done | bytes 65568 | tf_op jit(solution)/shard_map/all_to_all | solution.py:294
  69.5 1.1 %shard_map.100 = (f32[8,128]{1,0:T(8,128)S(1)}, f32[8,8,1024]{2,1,0:T(8,128)S(1)}, f32[16,8,128]{2,1,0:T(8,128)}) custom-call(f32[16,8,128]{2,1,0:T(8,128)S(1)} %all-to-all-done.arrived_ref, f32[8,128]{1,0:T(8,128)S(1)} %pad.4.s_ref, f32[8,128]{1,0:T(8,128)S(1)} %broadcast_in_dim.5.many_ref, f32[3,8,1024]{2,1,0:T(8,128)S(1)} %get-tuple-element.68.coadd_ref, ...), custom_call_target="tpu_custom_call" | custom-call | flops 4000000 | bytes 1000000 | tf_op jit(solution)/shard_map/pallas_call | solution.py:237
  70.7 4.7 %all-to-all-start.1 = ((f32[16,8,128]{2,1,0:T(8,128)}), f32[16,8,128]{2,1,0:T(8,128)S(1)}, u32[]{:S(2)}, u32[]{:S(2)}) async-start(f32[16,8,128]{2,1,0:T(8,128)} %get-tuple-element.72), calls=%async_computation.1 | async-start | bytes 131072 | tf_op jit(solution)/shard_map/all_to_all | solution.py:294
  75.4 0.7 copy.17
  76.2 5.6 %all-to-all-done.1.arrived_ref = f32[16,8,128]{2,1,0:T(8,128)S(1)} async-done(((f32[16,8,128]{2,1,0:T(8,128)}), f32[16,8,128]{2,1,0:T(8,128)S(1)}, u32[]{:S(2)}, u32[]{:S(2)}) %all-to-all-start.1) | async-done | bytes 65568 | tf_op jit(solution)/shard_map/all_to_all | solution.py:294
  81.8 0.8 shard_map.101
  (8 shorter events, 0.1 us)
Async XLA Ops:
  0.6 0.7 copy-start
  3.7 10.9 %collective-permute-start = (f32[2,3,8,1024]{3,2,1,0:T(8,128)S(1)}, f32[2,3,8,1024]{3,2,1,0:T(8,128)S(1)}, u32[]{:S(2)}, u32[]{:S(2)}) collective-permute-start(f32[2,3,8,1024]{3,2,1,0:T(8,128)S(1)} %get-tuple-element.43), channel_id=1, source_target_pairs={{0,48},{16,32},{32,16},{48,0},{64,112},{80,96},{96,80},{112,64},{1... | collective-permute-start | bytes 589832 | tf_op jit(solution)/shard_map/ppermute | solution.py:255
  5.3 9.4 %collective-permute-start.1 = (f32[2,3,8,1024]{3,2,1,0:T(8,128)S(1)}, f32[2,3,8,1024]{3,2,1,0:T(8,128)S(1)}, u32[]{:S(2)}, u32[]{:S(2)}) collective-permute-start(f32[2,3,8,1024]{3,2,1,0:T(8,128)S(1)} %get-tuple-element.45), channel_id=1, source_target_pairs={{0,16},{16,0},{32,48},{48,32},{64,80},{80,64},{96,112},{112,96},{1... | collective-permute-start | bytes 589832 | tf_op jit(solution)/shard_map/ppermute | solution.py:255
  9.4 27.4 %copy-start.4 = (s32[4]{0:T(128)S(1)}, s32[4]{0:T(128)}, u32[]{:S(2)}) copy-start(s32[4]{0:T(128)} %param.11) | copy-start | bytes 52
  9.5 34.1 %copy-start.1 = (f32[4,8,1024]{2,1,0:T(8,128)S(1)}, f32[4,8,1024]{2,1,0:T(8,128)}, u32[]{:S(2)}) copy-start(f32[4,8,1024]{2,1,0:T(8,128)} %param.13) | copy-start | bytes 393220
  9.5 34.1 %copy-start.2 = (s32[4,8,1024]{2,1,0:T(8,128)S(1)}, s32[4,8,1024]{2,1,0:T(8,128)}, u32[]{:S(2)}) copy-start(s32[4,8,1024]{2,1,0:T(8,128)} %param.10) | copy-start | bytes 393220
  9.5 34.3 %copy-start.3 = (f32[4,8,6]{1,0,2:T(4,128)S(1)}, f32[4,8,6]{1,0,2:T(4,128)}, u32[]{:S(2)}) copy-start(f32[4,8,6]{1,0,2:T(4,128)} %param.12) | copy-start | bytes 2308
  9.5 7.4 %collective-permute-start.8 = (f32[2,3,8,1024]{3,2,1,0:T(8,128)S(1)}, f32[2,3,8,1024]{3,2,1,0:T(8,128)S(1)}, u32[]{:S(2)}, u32[]{:S(2)}) collective-permute-start(f32[2,3,8,1024]{3,2,1,0:T(8,128)S(1)} %get-tuple-element.57), channel_id=1, source_target_pairs={{0,192},{16,208},{32,224},{48,240},{64,128},{80,144},{96,160},{112... | collective-permute-start | bytes 589832 | tf_op jit(solution)/shard_map/ppermute | solution.py:255
  12.6 7.8 %collective-permute-start.9 = (f32[2,3,8,1024]{3,2,1,0:T(8,128)S(1)}, f32[2,3,8,1024]{3,2,1,0:T(8,128)S(1)}, u32[]{:S(2)}, u32[]{:S(2)}) collective-permute-start(f32[2,3,8,1024]{3,2,1,0:T(8,128)S(1)} %get-tuple-element.59), channel_id=1, source_target_pairs={{0,64},{16,80},{32,96},{48,112},{64,0},{80,16},{96,32},{112,48},{1... | collective-permute-start | bytes 589832 | tf_op jit(solution)/shard_map/ppermute | solution.py:255
  12.7 9.9 %collective-permute-start.7 = (f32[2,3,8,1024]{3,2,1,0:T(8,128)S(1)}, f32[2,3,8,1024]{3,2,1,0:T(8,128)S(1)}, u32[]{:S(2)}, u32[]{:S(2)}) collective-permute-start(f32[2,3,8,1024]{3,2,1,0:T(8,128)S(1)} %get-tuple-element.55), channel_id=1, source_target_pairs={{0,64},{16,80},{32,96},{48,112},{64,0},{80,16},{96,32},{112,48},{1... | collective-permute-start | bytes 589832 | tf_op jit(solution)/shard_map/ppermute | solution.py:255
  14.7 17.8 %collective-permute-start.2 = (f32[4,3,8,1024]{3,2,1,0:T(8,128)S(1)}, f32[4,3,8,1024]{3,2,1,0:T(8,128)S(1)}, u32[]{:S(2)}, u32[]{:S(2)}) collective-permute-start(f32[4,3,8,1024]{3,2,1,0:T(8,128)S(1)} %get-tuple-element.47), channel_id=1, source_target_pairs={{0,16},{16,0},{32,48},{48,32},{64,80},{80,64},{96,112},{112,96},{1... | collective-permute-start | bytes 1179656 | tf_op jit(solution)/shard_map/ppermute | solution.py:255
  15.0 17.5 %collective-permute-start.3 = (f32[4,3,8,1024]{3,2,1,0:T(8,128)S(1)}, f32[4,3,8,1024]{3,2,1,0:T(8,128)S(1)}, u32[]{:S(2)}, u32[]{:S(2)}) collective-permute-start(f32[4,3,8,1024]{3,2,1,0:T(8,128)S(1)} %get-tuple-element.48), channel_id=1, source_target_pairs={{0,48},{16,32},{32,16},{48,0},{64,112},{80,96},{96,80},{112,64},{1... | collective-permute-start | bytes 1179656 | tf_op jit(solution)/shard_map/ppermute | solution.py:255
  16.9 8.7 %collective-permute-start.11 = (f32[2,3,8,1024]{3,2,1,0:T(8,128)S(1)}, f32[2,3,8,1024]{3,2,1,0:T(8,128)S(1)}, u32[]{:S(2)}, u32[]{:S(2)}) collective-permute-start(f32[2,3,8,1024]{3,2,1,0:T(8,128)S(1)} %get-tuple-element.62), channel_id=1, source_target_pairs={{0,192},{16,208},{32,224},{48,240},{64,128},{80,144},{96,160},{112... | collective-permute-start | bytes 589832 | tf_op jit(solution)/shard_map/ppermute | solution.py:255
  20.4 7.6 %collective-permute-start.10 = (f32[2,3,8,1024]{3,2,1,0:T(8,128)S(1)}, f32[2,3,8,1024]{3,2,1,0:T(8,128)S(1)}, u32[]{:S(2)}, u32[]{:S(2)}) collective-permute-start(f32[2,3,8,1024]{3,2,1,0:T(8,128)S(1)} %get-tuple-element.60), channel_id=1, source_target_pairs={{0,192},{16,208},{32,224},{48,240},{64,128},{80,144},{96,160},{112... | collective-permute-start | bytes 589832 | tf_op jit(solution)/shard_map/ppermute | solution.py:255
  22.6 5.7 %collective-permute-start.12 = (f32[2,3,8,1024]{3,2,1,0:T(8,128)S(1)}, f32[2,3,8,1024]{3,2,1,0:T(8,128)S(1)}, u32[]{:S(2)}, u32[]{:S(2)}) collective-permute-start(f32[2,3,8,1024]{3,2,1,0:T(8,128)S(1)} %get-tuple-element.63), channel_id=1, source_target_pairs={{0,64},{16,80},{32,96},{48,112},{64,0},{80,16},{96,32},{112,48},{1... | collective-permute-start | bytes 589832 | tf_op jit(solution)/shard_map/ppermute | solution.py:255
  28.3 7.5 %collective-permute-start.13 = (f32[3,8,1024]{2,1,0:T(8,128)S(1)}, f32[3,8,1024]{2,1,0:T(8,128)S(1)}, u32[]{:S(2)}, u32[]{:S(2)}) collective-permute-start(f32[3,8,1024]{2,1,0:T(8,128)S(1)} %get-tuple-element.65), channel_id=1, source_target_pairs={{0,32},{16,48},{32,0},{48,16},{64,96},{80,112},{96,64},{112,80},{1... | collective-permute-start | bytes 294920 | tf_op jit(solution)/shard_map/ppermute | solution.py:255
  29.1 7.7 %collective-permute-start.14 = (f32[3,8,1024]{2,1,0:T(8,128)S(1)}, f32[3,8,1024]{2,1,0:T(8,128)S(1)}, u32[]{:S(2)}, u32[]{:S(2)}) collective-permute-start(f32[3,8,1024]{2,1,0:T(8,128)S(1)} %get-tuple-element.66), channel_id=1, source_target_pairs={{0,16},{16,0},{32,48},{48,32},{64,80},{80,64},{96,112},{112,96},{1... | collective-permute-start | bytes 294920 | tf_op jit(solution)/shard_map/ppermute | solution.py:255
  30.4 6.5 %collective-permute-start.15 = (f32[3,8,1024]{2,1,0:T(8,128)S(1)}, f32[3,8,1024]{2,1,0:T(8,128)S(1)}, u32[]{:S(2)}, u32[]{:S(2)}) collective-permute-start(f32[3,8,1024]{2,1,0:T(8,128)S(1)} %get-tuple-element.67), channel_id=1, source_target_pairs={{0,48},{16,32},{32,16},{48,0},{64,112},{80,96},{96,80},{112,64},{1... | collective-permute-start | bytes 294920 | tf_op jit(solution)/shard_map/ppermute | solution.py:255
  32.6 6.2 %collective-permute-start.4 = (f32[3,8,1024]{2,1,0:T(8,128)S(1)}, f32[3,8,1024]{2,1,0:T(8,128)S(1)}, u32[]{:S(2)}, u32[]{:S(2)}) collective-permute-start(f32[3,8,1024]{2,1,0:T(8,128)S(1)} %get-tuple-element.50), channel_id=1, source_target_pairs={{0,128},{16,144},{32,160},{48,176},{64,192},{80,208},{96,224},{112... | collective-permute-start | bytes 294920 | tf_op jit(solution)/shard_map/ppermute | solution.py:255
  33.3 6.1 %collective-permute-start.5 = (f32[3,8,1024]{2,1,0:T(8,128)S(1)}, f32[3,8,1024]{2,1,0:T(8,128)S(1)}, u32[]{:S(2)}, u32[]{:S(2)}) collective-permute-start(f32[3,8,1024]{2,1,0:T(8,128)S(1)} %get-tuple-element.51), channel_id=1, source_target_pairs={{0,64},{16,80},{32,96},{48,112},{64,0},{80,16},{96,32},{112,48},{1... | collective-permute-start | bytes 294920 | tf_op jit(solution)/shard_map/ppermute | solution.py:255
  35.8 5.8 %collective-permute-start.6 = (f32[3,8,1024]{2,1,0:T(8,128)S(1)}, f32[3,8,1024]{2,1,0:T(8,128)S(1)}, u32[]{:S(2)}, u32[]{:S(2)}) collective-permute-start(f32[3,8,1024]{2,1,0:T(8,128)S(1)} %get-tuple-element.52), channel_id=1, source_target_pairs={{0,192},{16,208},{32,224},{48,240},{64,128},{80,144},{96,160},{112... | collective-permute-start | bytes 294920 | tf_op jit(solution)/shard_map/ppermute | solution.py:255
  41.7 8.5 %collective-permute-start.16 = (f32[6,8,1024]{2,1,0:T(8,128)S(1)}, f32[6,8,1024]{2,1,0:T(8,128)S(1)}, u32[]{:S(2)}, u32[]{:S(2)}) collective-permute-start(f32[6,8,1024]{2,1,0:T(8,128)S(1)} %shard_map.98), channel_id=1, source_target_pairs={{0,0},{1,25},{2,46},{3,55},{4,76},{5,85},{6,106},{7,115},{8,136},{... | collective-permute-start | bytes 589832 | tf_op jit(solution)/shard_map/ppermute | solution.py:278
  51.3 18.2 %all-to-all-start = ((f32[16,8,128]{2,1,0:T(8,128)}), f32[16,8,128]{2,1,0:T(8,128)S(1)}, u32[]{:S(2)}, u32[]{:S(2)}) async-start(f32[16,8,128]{2,1,0:T(8,128)} %get-tuple-element.69), calls=%async_computation | async-start | bytes 131072 | tf_op jit(solution)/shard_map/all_to_all | solution.py:294
  70.7 11.1 %all-to-all-start.1 = ((f32[16,8,128]{2,1,0:T(8,128)}), f32[16,8,128]{2,1,0:T(8,128)S(1)}, u32[]{:S(2)}, u32[]{:S(2)}) async-start(f32[16,8,128]{2,1,0:T(8,128)} %get-tuple-element.72), calls=%async_computation.1 | async-start | bytes 131072 | tf_op jit(solution)/shard_map/all_to_all | solution.py:294
where the time goes:
time: 84.2 us; the launch traced here: 82.5 us
  starting transfers between devices  39.9 us (47%)
  waiting for transfers between devices  31.2 us (37%)
  Pallas kernels  7.98 us (9%)
  local copies, waits for them, and re-layouts  2.37 us (3%)
    ppermute x16, starting transfers between devices, hop(): return lax.ppermute(a, 'epoch', [(e, e ^ m) for e in range(n_epoch)])  21.3 us
    all_to_all x2, starting transfers between devices, on_device(): lax.all_to_all(a, 'epoch', split_axis=0, concat_axis=0, tiled=True)  16.7 us
    ppermute x16, waiting for transfers between devices, hop(): return lax.ppermute(a, 'epoch', [(e, e ^ m) for e in range(n_epoch)])  13.9 us
    all_to_all x2, waiting for transfers between devices, on_device(): lax.all_to_all(a, 'epoch', split_axis=0, concat_axis=0, tiled=True)  11.2 us
    ppermute x1, waiting for transfers between devices, on_device(): sums = lax.ppermute(total, ('epoch', 'blend'), home)  6.05 us
    pallas_call x2, Pallas kernels, visit_sums(): pl.pallas_call(lambda *refs: visit_kernel(first, *refs), out_shape=outs,...  4.74 us
    pallas_call x8, Pallas kernels, call(): pl.pallas_call(kernel, out_shape=[jax.ShapeDtypeStruct(o, F32) for o in o...  3.25 us
    ppermute x1, starting transfers between devices, on_device(): sums = lax.ppermute(total, ('epoch', 'blend'), home)  1.92 us
  transfers between devices with their start and end apart: 19, of which 12 were waited for; matrix products, arithmetic and copies ran while one was open for 2% of the time, Pallas kernels for 3%

commit v1 on v0

--- a/solution.py
+++ b/solution.py
@@ -12,8 +12,28 @@
 ANY = pl.BlockSpec(memory_space=pl.ANY)
 
 
+PAIRS = (
+    0x15742603,
+    0x63521407,
+    0x50123746,
+    0x61274053,
+    0x46231570,
+    0x40375261,
+    0x34261570,
+    0x03624715,
+    0x21654037,
+    0x54306127,
+    0x47120653,
+    0x12705463,
+    0x41567320,
+    0x02763514,
+    0x70154236,
+    0x75340162,
+)
+
+
 def held_group(e, i):
-    return 2 * ((e // 2 + 4 * (i % 2) - i // 2) % 8) + (e + i) % 2
+    return 2 * (PAIRS[i] >> 4 * (e // 2) & 7) + (e + i) % 2
 
 
 def visit_kernel(first, flux_ref, prec_ref, live_ref, *rest):
@@ -23,6 +43,9 @@
         outs, (flux_buf, prec_buf, sems) = rest[:8], rest[8:]
     e, i = lax.axis_index("epoch"), lax.axis_index("blend")
     odd = lax.rem(e + i, 2) == 1
+    held = jnp.int32(PAIRS[0])
+    for n in range(1, len(PAIRS)):
+        held = jnp.where(i == n, PAIRS[n], held)
     bands, visits, tiles = flux_buf.shape[:3]
     width = flux_buf.shape[4]
     base = 0 if first else bands
@@ -53,7 +76,7 @@
         for copy in copies[c]:
             copy.wait()
         for j in range(tiles):
-            pair = lax.rem(lax.bitwise_xor(lax.div(e, 2), j) + 4 * lax.rem(i, 2) + 8 - lax.div(i, 2), 8)
+            pair = lax.bitwise_and(lax.shift_right_logical(held, 4 * lax.bitwise_xor(lax.div(e, 2), j)), 7)
             lives = [live[v, pair] for v in range(visits)]
             x, y = 2 * (j % 2), j // 2
             (far0, far1), (at0, at1) = ((x, x + 1), (y, y)) if first else ((y, y), (x, x + 1))
@@ -273,7 +296,7 @@
     a = call(join_all_kernel, [piece] * 4, [a[0], a[1], *a_last], ())
     a = [a[0]] + [hop(a[m], 4 * m) for m in (2, 1, 3)]
     b = call(join_kernel, [piece] * 4, [b[0], b_near[0], b_last[1], b[1], b_near[1], b_last[0]], ())
-    b = [b[0]] + [hop(b[m], m) for m in (2, 1, 3)]
+    b = [b[0]] + [hop(b[m], m) for m in (1, 3, 2)]
     (total,) = call(total_kernel, [(bands, 8, width)], [*a, *b], ())
     sums = lax.ppermute(total, ("epoch", "blend"), home)
 

time: 84.2 us -> 83.6 us (level); the launches traced: 82.5 us -> 83 us
  no operation moved by 1% of the time
where the time goes in v1:
time: 83.6 us; the launch traced here: 83 us
  starting transfers between devices  40.3 us (48%)
  waiting for transfers between devices  31.3 us (37%)
  Pallas kernels  7.98 us (10%)
  local copies, waits for them, and re-layouts  2.37 us (3%)
    ppermute x16, starting transfers between devices, hop(): return lax.ppermute(a, 'epoch', [(e, e ^ m) for e in range(n_epoch)])  21.3 us
    all_to_all x2, starting transfers between devices, on_device(): lax.all_to_all(a, 'epoch', split_axis=0, concat_axis=0, tiled=True)  17.1 us
    ppermute x16, waiting for transfers between devices, hop(): return lax.ppermute(a, 'epoch', [(e, e ^ m) for e in range(n_epoch)])  14 us
    all_to_all x2, waiting for transfers between devices, on_device(): lax.all_to_all(a, 'epoch', split_axis=0, concat_axis=0, tiled=True)  11.2 us
    ppermute x1, waiting for transfers between devices, on_device(): sums = lax.ppermute(total, ('epoch', 'blend'), home)  6.05 us
    pallas_call x2, Pallas kernels, visit_sums(): pl.pallas_call(lambda *refs: visit_kernel(first, *refs), out_shape=outs,...  4.73 us
    pallas_call x8, Pallas kernels, call(): pl.pallas_call(kernel, out_shape=[jax.ShapeDtypeStruct(o, F32) for o in o...  3.25 us
    ppermute x1, starting transfers between devices, on_device(): sums = lax.ppermute(total, ('epoch', 'blend'), home)  1.92 us
  transfers between devices with their start and end apart: 19, of which 12 were waited for; matrix products, arithmetic and copies ran while one was open for 2% of the time, Pallas kernels for 3%

profile of v1, /device:TPU:2, one launch (start us, length us, event | category | flops | bytes accessed | tf_op | source)
XLA Modules:
  0.0 83.0 jit_solution(11025661012231334983)
XLA Ops:
  0.6 0.0 copy-start
  0.6 0.7 copy-done
  1.3 2.4 %visit_first.1 = (f32[2,3,8,1024]{3,2,1,0:T(8,128)S(1)}, f32[2,3,8,1024]{3,2,1,0:T(8,128)S(1)}, f32[2,3,8,1024]{3,2,1,0:T(8,128)S(1)}, f32[2,3,8,1024]{3,2,1,0:T...) custom-call(bf16[4,6,8,8,1024]{4,3,2,1,0:T(8,128)(2,1)} %bitcast.18,, ...), custom_call_target="tpu_custom_call" | custom-call | flops 6291456 | bytes 3145728 | tf_op jit(solution)/shard_map/visit_first/pallas_call | solution.py:112
  3.7 1.6 %collective-permute-start = (f32[2,3,8,1024]{3,2,1,0:T(8,128)S(1)}, f32[2,3,8,1024]{3,2,1,0:T(8,128)S(1)}, u32[]{:S(2)}, u32[]{:S(2)}) collective-permute-start(f32[2,3,8,1024]{3,2,1,0:T(8,128)S(1)} %get-tuple-element.43), channel_id=1, source_target_pairs={{0,48},{16,32},{32,16},{48,0},{64,112},{80,96},{96,80},{112,64},{1... | collective-permute-start | bytes 589832 | tf_op jit(solution)/shard_map/ppermute | solution.py:278
  5.3 1.8 %collective-permute-start.1 = (f32[2,3,8,1024]{3,2,1,0:T(8,128)S(1)}, f32[2,3,8,1024]{3,2,1,0:T(8,128)S(1)}, u32[]{:S(2)}, u32[]{:S(2)}) collective-permute-start(f32[2,3,8,1024]{3,2,1,0:T(8,128)S(1)} %get-tuple-element.45), channel_id=1, source_target_pairs={{0,16},{16,0},{32,48},{48,32},{64,80},{80,64},{96,112},{112,96},{1... | collective-permute-start | bytes 589832 | tf_op jit(solution)/shard_map/ppermute | solution.py:278
  7.1 2.4 %visit_second.1 = (f32[2,3,8,1024]{3,2,1,0:T(8,128)S(1)}, f32[2,3,8,1024]{3,2,1,0:T(8,128)S(1)}, f32[2,3,8,1024]{3,2,1,0:T(8,128)S(1)}, f32[2,3,8,1024]{3,2,1,0:...) custom-call(bf16[4,6,8,8,1024]{4,3,2,1,0:T(8,128)(2,1)} %bitcast.19,, ...), custom_call_target="tpu_custom_call" | custom-call | flops 6291456 | bytes 3145728 | tf_op jit(solution)/shard_map/visit_second/pallas_call | solution.py:112
  9.4 0.0 copy-start.4
  9.5 0.0 copy-start.1
  9.5 0.0 copy-start.2
  9.5 0.0 copy-start.3
  9.5 3.1 %collective-permute-start.8 = (f32[2,3,8,1024]{3,2,1,0:T(8,128)S(1)}, f32[2,3,8,1024]{3,2,1,0:T(8,128)S(1)}, u32[]{:S(2)}, u32[]{:S(2)}) collective-permute-start(f32[2,3,8,1024]{3,2,1,0:T(8,128)S(1)} %get-tuple-element.57), channel_id=1, source_target_pairs={{0,192},{16,208},{32,224},{48,240},{64,128},{80,144},{96,160},{112... | collective-permute-start | bytes 589832 | tf_op jit(solution)/shard_map/ppermute | solution.py:278
  12.6 0.1 collective-permute-start.9
  12.7 1.9 %collective-permute-start.7 = (f32[2,3,8,1024]{3,2,1,0:T(8,128)S(1)}, f32[2,3,8,1024]{3,2,1,0:T(8,128)S(1)}, u32[]{:S(2)}, u32[]{:S(2)}) collective-permute-start(f32[2,3,8,1024]{3,2,1,0:T(8,128)S(1)} %get-tuple-element.55), channel_id=1, source_target_pairs={{0,64},{16,80},{32,96},{48,112},{64,0},{80,16},{96,32},{112,48},{1... | collective-permute-start | bytes 589832 | tf_op jit(solution)/shard_map/ppermute | solution.py:278
  14.6 0.0 collective-permute-done.far1
  14.6 0.0 collective-permute-done.1.far0
  14.6 0.1 shard_map.94
  14.7 0.3 collective-permute-start.2
  15.0 0.5 collective-permute-start.3
  15.5 1.4 %collective-permute-done.8.b = f32[2,3,8,1024]{3,2,1,0:T(8,128)S(1)} collective-permute-done((f32[2,3,8,1024]{3,2,1,0:T(8,128)S(1)}, f32[2,3,8,1024]{3,2,1,0:T(8,128)S(1)}, u32[]{:S(2)}, u32[]{:S(2)}) %collective-permute-start.8) | collective-permute-done | bytes 196640 | tf_op jit(solution)/shard_map/ppermute | solution.py:278
  16.9 3.0 %collective-permute-start.11 = (f32[2,3,8,1024]{3,2,1,0:T(8,128)S(1)}, f32[2,3,8,1024]{3,2,1,0:T(8,128)S(1)}, u32[]{:S(2)}, u32[]{:S(2)}) collective-permute-start(f32[2,3,8,1024]{3,2,1,0:T(8,128)S(1)} %get-tuple-element.62), channel_id=1, source_target_pairs={{0,192},{16,208},{32,224},{48,240},{64,128},{80,144},{96,160},{112... | collective-permute-start | bytes 589832 | tf_op jit(solution)/shard_map/ppermute | solution.py:278
  19.9 0.5 collective-permute-done.9.d
  20.4 0.3 collective-permute-start.10
  20.7 1.9 %collective-permute-done.7.refs_1_ = f32[2,3,8,1024]{3,2,1,0:T(8,128)S(1)} collective-permute-done((f32[2,3,8,1024]{3,2,1,0:T(8,128)S(1)}, f32[2,3,8,1024]{3,2,1,0:T(8,128)S(1)}, u32[]{:S(2)}, u32[]{:S(2)}) %collective-permute-start.7) | collective-permute-done | bytes 196640 | tf_op jit(solution)/shard_map/ppermute | solution.py:278
  22.6 0.3 collective-permute-start.12
  22.9 2.8 %collective-permute-done.11.refs_4_ = f32[2,3,8,1024]{3,2,1,0:T(8,128)S(1)} collective-permute-done((f32[2,3,8,1024]{3,2,1,0:T(8,128)S(1)}, f32[2,3,8,1024]{3,2,1,0:T(8,128)S(1)}, u32[]{:S(2)}, u32[]{:S(2)}) %collective-permute-start.11) | collective-permute-done | bytes 196640 | tf_op jit(solution)/shard_map/ppermute | solution.py:278
  25.7 2.4 %collective-permute-done.10.refs_2_ = f32[2,3,8,1024]{3,2,1,0:T(8,128)S(1)} collective-permute-done((f32[2,3,8,1024]{3,2,1,0:T(8,128)S(1)}, f32[2,3,8,1024]{3,2,1,0:T(8,128)S(1)}, u32[]{:S(2)}, u32[]{:S(2)}) %collective-permute-start.10) | collective-permute-done | bytes 196640 | tf_op jit(solution)/shard_map/ppermute | solution.py:278
  28.0 0.2 collective-permute-done.12.refs_5_
  28.3 0.1 shard_map.97
  28.3 0.4 collective-permute-start.13
  28.7 1.0 %collective-permute-start.14 = (f32[3,8,1024]{2,1,0:T(8,128)S(1)}, f32[3,8,1024]{2,1,0:T(8,128)S(1)}, u32[]{:S(2)}, u32[]{:S(2)}) collective-permute-start(f32[3,8,1024]{2,1,0:T(8,128)S(1)} %get-tuple-element.66), channel_id=1, source_target_pairs={{0,48},{16,32},{32,16},{48,0},{64,112},{80,96},{96,80},{112,64},{1... | collective-permute-start | bytes 294920 | tf_op jit(solution)/shard_map/ppermute | solution.py:278
  29.7 2.8 %collective-permute-start.15 = (f32[3,8,1024]{2,1,0:T(8,128)S(1)}, f32[3,8,1024]{2,1,0:T(8,128)S(1)}, u32[]{:S(2)}, u32[]{:S(2)}) collective-permute-start(f32[3,8,1024]{2,1,0:T(8,128)S(1)} %get-tuple-element.67), channel_id=1, source_target_pairs={{0,32},{16,48},{32,0},{48,16},{64,96},{80,112},{96,64},{112,80},{1... | collective-permute-start | bytes 294920 | tf_op jit(solution)/shard_map/ppermute | solution.py:278
  32.5 0.0 collective-permute-done.2.low
  32.5 0.0 collective-permute-done.3.high
  32.5 0.1 shard_map.95
  32.6 0.7 collective-permute-start.4
  33.3 2.5 %collective-permute-start.5 = (f32[3,8,1024]{2,1,0:T(8,128)S(1)}, f32[3,8,1024]{2,1,0:T(8,128)S(1)}, u32[]{:S(2)}, u32[]{:S(2)}) collective-permute-start(f32[3,8,1024]{2,1,0:T(8,128)S(1)} %get-tuple-element.51), channel_id=1, source_target_pairs={{0,64},{16,80},{32,96},{48,112},{64,0},{80,16},{96,32},{112,48},{1... | collective-permute-start | bytes 294920 | tf_op jit(solution)/shard_map/ppermute | solution.py:278
  35.8 0.0 collective-permute-done.13.refs_5_
  35.8 1.0 %collective-permute-start.6 = (f32[3,8,1024]{2,1,0:T(8,128)S(1)}, f32[3,8,1024]{2,1,0:T(8,128)S(1)}, u32[]{:S(2)}, u32[]{:S(2)}) collective-permute-start(f32[3,8,1024]{2,1,0:T(8,128)S(1)} %get-tuple-element.52), channel_id=1, source_target_pairs={{0,192},{16,208},{32,224},{48,240},{64,128},{80,144},{96,160},{112... | collective-permute-start | bytes 294920 | tf_op jit(solution)/shard_map/ppermute | solution.py:278
  36.8 0.0 copy-done.4
  36.8 0.0 collective-permute-done.14.refs_6_
  36.8 0.0 collective-permute-done.15.refs_7_
  36.8 2.0 %collective-permute-done.4.refs_1_ = f32[3,8,1024]{2,1,0:T(8,128)S(1)} collective-permute-done((f32[3,8,1024]{2,1,0:T(8,128)S(1)}, f32[3,8,1024]{2,1,0:T(8,128)S(1)}, u32[]{:S(2)}, u32[]{:S(2)}) %collective-permute-start.4) | collective-permute-done | bytes 98336 | tf_op jit(solution)/shard_map/ppermute | solution.py:278
  38.8 0.6 collective-permute-done.5.refs_2_
  39.4 2.2 %collective-permute-done.6.refs_3_ = f32[3,8,1024]{2,1,0:T(8,128)S(1)} collective-permute-done((f32[3,8,1024]{2,1,0:T(8,128)S(1)}, f32[3,8,1024]{2,1,0:T(8,128)S(1)}, u32[]{:S(2)}, u32[]{:S(2)}) %collective-permute-start.6) | collective-permute-done | bytes 98336 | tf_op jit(solution)/shard_map/ppermute | solution.py:278
  41.7 1.9 %collective-permute-start.16 = (f32[6,8,1024]{2,1,0:T(8,128)S(1)}, f32[6,8,1024]{2,1,0:T(8,128)S(1)}, u32[]{:S(2)}, u32[]{:S(2)}) collective-permute-start(f32[6,8,1024]{2,1,0:T(8,128)S(1)} %shard_map.98), channel_id=1, source_target_pairs={{0,6},{1,31},{2,44},{3,55},{4,64},{5,83},{6,96},{7,123},{8,142},{9... | collective-permute-start | bytes 589832 | tf_op jit(solution)/shard_map/ppermute | solution.py:301
  43.6 0.0 copy-done.1
  43.6 0.0 copy-done.2
  43.6 0.2 fusion
  43.8 0.0 copy-done.3
  43.8 0.1 reshape.48
  43.9 0.1 broadcast_in_dim.4
  44.0 0.1 pad_maximum_fusion
  44.1 6.1 %collective-permute-done.16.sums_ref = f32[6,8,1024]{2,1,0:T(8,128)S(1)} collective-permute-done((f32[6,8,1024]{2,1,0:T(8,128)S(1)}, f32[6,8,1024]{2,1,0:T(8,128)S(1)}, u32[]{:S(2)}, u32[]{:S(2)}) %collective-permute-start.16) | collective-permute-done | bytes 196640 | tf_op jit(solution)/shard_map/ppermute | solution.py:301
  50.2 0.1 broadcast_in_dim.5.many_ref
  50.2 1.1 %shard_map.99 = (f32[3,8,1024]{2,1,0:T(8,128)S(1)}, f32[3,8,1024]{2,1,0:T(8,128)S(1)}, f32[8,8,1024]{2,1,0:T(8,128)S(1)}, f32[16,8,128]{2,1,0:T(8,128)}) custom-call(f32[6,8,1024]{2,1,0:T(8,128)S(1)} %collective-permute-done.16.sums_ref, f32[8,8,1024]{2,1,0:T(8,128)S(1)} %get-tuple-element.83.mask_ref, f32[8,8,1024]{2,1,0:T(8,128)S(1)} %get-tuple-element.84.morph_ref, ...), custom_call_target="tpu_custom_call" | custom-call | flops 4000000 | bytes 1000000 | tf_op jit(solution)/shard_map/pallas_call | solution.py:260
  51.3 12.3 %all-to-all-start = ((f32[16,8,128]{2,1,0:T(8,128)}), f32[16,8,128]{2,1,0:T(8,128)S(1)}, u32[]{:S(2)}, u32[]{:S(2)}) async-start(f32[16,8,128]{2,1,0:T(8,128)} %get-tuple-element.69), calls=%async_computation | async-start | bytes 131072 | tf_op jit(solution)/shard_map/all_to_all | solution.py:317
  63.6 0.7 reshape.49
  64.3 5.6 %all-to-all-done.arrived_ref = f32[16,8,128]{2,1,0:T(8,128)S(1)} async-done(((f32[16,8,128]{2,1,0:T(8,128)}), f32[16,8,128]{2,1,0:T(8,128)S(1)}, u32[]{:S(2)}, u32[]{:S(2)}) %all-to-all-start) | async-done | bytes 65568 | tf_op jit(solution)/shard_map/all_to_all | solution.py:317
  69.9 1.1 %shard_map.100 = (f32[8,128]{1,0:T(8,128)S(1)}, f32[8,8,1024]{2,1,0:T(8,128)S(1)}, f32[16,8,128]{2,1,0:T(8,128)}) custom-call(f32[16,8,128]{2,1,0:T(8,128)S(1)} %all-to-all-done.arrived_ref, f32[8,128]{1,0:T(8,128)S(1)} %pad.4.s_ref, f32[8,128]{1,0:T(8,128)S(1)} %broadcast_in_dim.5.many_ref, f32[3,8,1024]{2,1,0:T(8,128)S(1)} %get-tuple-element.68.coadd_ref, ...), custom_call_target="tpu_custom_call" | custom-call | flops 4000000 | bytes 1000000 | tf_op jit(solution)/shard_map/pallas_call | solution.py:260
  71.1 4.7 %all-to-all-start.1 = ((f32[16,8,128]{2,1,0:T(8,128)}), f32[16,8,128]{2,1,0:T(8,128)S(1)}, u32[]{:S(2)}, u32[]{:S(2)}) async-start(f32[16,8,128]{2,1,0:T(8,128)} %get-tuple-element.72), calls=%async_computation.1 | async-start | bytes 131072 | tf_op jit(solution)/shard_map/all_to_all | solution.py:317
  75.9 0.7 copy.17
  76.6 5.6 %all-to-all-done.1.arrived_ref = f32[16,8,128]{2,1,0:T(8,128)S(1)} async-done(((f32[16,8,128]{2,1,0:T(8,128)}), f32[16,8,128]{2,1,0:T(8,128)S(1)}, u32[]{:S(2)}, u32[]{:S(2)}) %all-to-all-start.1) | async-done | bytes 65568 | tf_op jit(solution)/shard_map/all_to_all | solution.py:317
  82.2 0.8 shard_map.101
  (8 shorter events, 0.1 us)
Async XLA Ops:
  0.6 0.7 copy-start
  3.7 10.9 %collective-permute-start = (f32[2,3,8,1024]{3,2,1,0:T(8,128)S(1)}, f32[2,3,8,1024]{3,2,1,0:T(8,128)S(1)}, u32[]{:S(2)}, u32[]{:S(2)}) collective-permute-start(f32[2,3,8,1024]{3,2,1,0:T(8,128)S(1)} %get-tuple-element.43), channel_id=1, source_target_pairs={{0,48},{16,32},{32,16},{48,0},{64,112},{80,96},{96,80},{112,64},{1... | collective-permute-start | bytes 589832 | tf_op jit(solution)/shard_map/ppermute | solution.py:278
  5.3 9.4 %collective-permute-start.1 = (f32[2,3,8,1024]{3,2,1,0:T(8,128)S(1)}, f32[2,3,8,1024]{3,2,1,0:T(8,128)S(1)}, u32[]{:S(2)}, u32[]{:S(2)}) collective-permute-start(f32[2,3,8,1024]{3,2,1,0:T(8,128)S(1)} %get-tuple-element.45), channel_id=1, source_target_pairs={{0,16},{16,0},{32,48},{48,32},{64,80},{80,64},{96,112},{112,96},{1... | collective-permute-start | bytes 589832 | tf_op jit(solution)/shard_map/ppermute | solution.py:278
  9.4 27.3 %copy-start.4 = (s32[4]{0:T(128)S(1)}, s32[4]{0:T(128)}, u32[]{:S(2)}) copy-start(s32[4]{0:T(128)} %param.11) | copy-start | bytes 52
  9.5 34.1 %copy-start.1 = (f32[4,8,1024]{2,1,0:T(8,128)S(1)}, f32[4,8,1024]{2,1,0:T(8,128)}, u32[]{:S(2)}) copy-start(f32[4,8,1024]{2,1,0:T(8,128)} %param.13) | copy-start | bytes 393220
  9.5 34.1 %copy-start.2 = (s32[4,8,1024]{2,1,0:T(8,128)S(1)}, s32[4,8,1024]{2,1,0:T(8,128)}, u32[]{:S(2)}) copy-start(s32[4,8,1024]{2,1,0:T(8,128)} %param.10) | copy-start | bytes 393220
  9.5 34.3 %copy-start.3 = (f32[4,8,6]{1,0,2:T(4,128)S(1)}, f32[4,8,6]{1,0,2:T(4,128)}, u32[]{:S(2)}) copy-start(f32[4,8,6]{1,0,2:T(4,128)} %param.12) | copy-start | bytes 2308
  9.5 7.4 %collective-permute-start.8 = (f32[2,3,8,1024]{3,2,1,0:T(8,128)S(1)}, f32[2,3,8,1024]{3,2,1,0:T(8,128)S(1)}, u32[]{:S(2)}, u32[]{:S(2)}) collective-permute-start(f32[2,3,8,1024]{3,2,1,0:T(8,128)S(1)} %get-tuple-element.57), channel_id=1, source_target_pairs={{0,192},{16,208},{32,224},{48,240},{64,128},{80,144},{96,160},{112... | collective-permute-start | bytes 589832 | tf_op jit(solution)/shard_map/ppermute | solution.py:278
  12.6 7.8 %collective-permute-start.9 = (f32[2,3,8,1024]{3,2,1,0:T(8,128)S(1)}, f32[2,3,8,1024]{3,2,1,0:T(8,128)S(1)}, u32[]{:S(2)}, u32[]{:S(2)}) collective-permute-start(f32[2,3,8,1024]{3,2,1,0:T(8,128)S(1)} %get-tuple-element.59), channel_id=1, source_target_pairs={{0,64},{16,80},{32,96},{48,112},{64,0},{80,16},{96,32},{112,48},{1... | collective-permute-start | bytes 589832 | tf_op jit(solution)/shard_map/ppermute | solution.py:278
  12.7 9.9 %collective-permute-start.7 = (f32[2,3,8,1024]{3,2,1,0:T(8,128)S(1)}, f32[2,3,8,1024]{3,2,1,0:T(8,128)S(1)}, u32[]{:S(2)}, u32[]{:S(2)}) collective-permute-start(f32[2,3,8,1024]{3,2,1,0:T(8,128)S(1)} %get-tuple-element.55), channel_id=1, source_target_pairs={{0,64},{16,80},{32,96},{48,112},{64,0},{80,16},{96,32},{112,48},{1... | collective-permute-start | bytes 589832 | tf_op jit(solution)/shard_map/ppermute | solution.py:278
  14.7 17.8 %collective-permute-start.2 = (f32[4,3,8,1024]{3,2,1,0:T(8,128)S(1)}, f32[4,3,8,1024]{3,2,1,0:T(8,128)S(1)}, u32[]{:S(2)}, u32[]{:S(2)}) collective-permute-start(f32[4,3,8,1024]{3,2,1,0:T(8,128)S(1)} %get-tuple-element.47), channel_id=1, source_target_pairs={{0,16},{16,0},{32,48},{48,32},{64,80},{80,64},{96,112},{112,96},{1... | collective-permute-start | bytes 1179656 | tf_op jit(solution)/shard_map/ppermute | solution.py:278
  15.0 17.5 %collective-permute-start.3 = (f32[4,3,8,1024]{3,2,1,0:T(8,128)S(1)}, f32[4,3,8,1024]{3,2,1,0:T(8,128)S(1)}, u32[]{:S(2)}, u32[]{:S(2)}) collective-permute-start(f32[4,3,8,1024]{3,2,1,0:T(8,128)S(1)} %get-tuple-element.48), channel_id=1, source_target_pairs={{0,48},{16,32},{32,16},{48,0},{64,112},{80,96},{96,80},{112,64},{1... | collective-permute-start | bytes 1179656 | tf_op jit(solution)/shard_map/ppermute | solution.py:278
  16.9 8.7 %collective-permute-start.11 = (f32[2,3,8,1024]{3,2,1,0:T(8,128)S(1)}, f32[2,3,8,1024]{3,2,1,0:T(8,128)S(1)}, u32[]{:S(2)}, u32[]{:S(2)}) collective-permute-start(f32[2,3,8,1024]{3,2,1,0:T(8,128)S(1)} %get-tuple-element.62), channel_id=1, source_target_pairs={{0,192},{16,208},{32,224},{48,240},{64,128},{80,144},{96,160},{112... | collective-permute-start | bytes 589832 | tf_op jit(solution)/shard_map/ppermute | solution.py:278
  20.4 7.6 %collective-permute-start.10 = (f32[2,3,8,1024]{3,2,1,0:T(8,128)S(1)}, f32[2,3,8,1024]{3,2,1,0:T(8,128)S(1)}, u32[]{:S(2)}, u32[]{:S(2)}) collective-permute-start(f32[2,3,8,1024]{3,2,1,0:T(8,128)S(1)} %get-tuple-element.60), channel_id=1, source_target_pairs={{0,192},{16,208},{32,224},{48,240},{64,128},{80,144},{96,160},{112... | collective-permute-start | bytes 589832 | tf_op jit(solution)/shard_map/ppermute | solution.py:278
  22.6 5.7 %collective-permute-start.12 = (f32[2,3,8,1024]{3,2,1,0:T(8,128)S(1)}, f32[2,3,8,1024]{3,2,1,0:T(8,128)S(1)}, u32[]{:S(2)}, u32[]{:S(2)}) collective-permute-start(f32[2,3,8,1024]{3,2,1,0:T(8,128)S(1)} %get-tuple-element.63), channel_id=1, source_target_pairs={{0,64},{16,80},{32,96},{48,112},{64,0},{80,16},{96,32},{112,48},{1... | collective-permute-start | bytes 589832 | tf_op jit(solution)/shard_map/ppermute | solution.py:278
  28.3 7.5 %collective-permute-start.13 = (f32[3,8,1024]{2,1,0:T(8,128)S(1)}, f32[3,8,1024]{2,1,0:T(8,128)S(1)}, u32[]{:S(2)}, u32[]{:S(2)}) collective-permute-start(f32[3,8,1024]{2,1,0:T(8,128)S(1)} %get-tuple-element.65), channel_id=1, source_target_pairs={{0,16},{16,0},{32,48},{48,32},{64,80},{80,64},{96,112},{112,96},{1... | collective-permute-start | bytes 294920 | tf_op jit(solution)/shard_map/ppermute | solution.py:278
  28.7 8.1 %collective-permute-start.14 = (f32[3,8,1024]{2,1,0:T(8,128)S(1)}, f32[3,8,1024]{2,1,0:T(8,128)S(1)}, u32[]{:S(2)}, u32[]{:S(2)}) collective-permute-start(f32[3,8,1024]{2,1,0:T(8,128)S(1)} %get-tuple-element.66), channel_id=1, source_target_pairs={{0,48},{16,32},{32,16},{48,0},{64,112},{80,96},{96,80},{112,64},{1... | collective-permute-start | bytes 294920 | tf_op jit(solution)/shard_map/ppermute | solution.py:278
  29.7 7.1 %collective-permute-start.15 = (f32[3,8,1024]{2,1,0:T(8,128)S(1)}, f32[3,8,1024]{2,1,0:T(8,128)S(1)}, u32[]{:S(2)}, u32[]{:S(2)}) collective-permute-start(f32[3,8,1024]{2,1,0:T(8,128)S(1)} %get-tuple-element.67), channel_id=1, source_target_pairs={{0,32},{16,48},{32,0},{48,16},{64,96},{80,112},{96,64},{112,80},{1... | collective-permute-start | bytes 294920 | tf_op jit(solution)/shard_map/ppermute | solution.py:278
  32.6 6.2 %collective-permute-start.4 = (f32[3,8,1024]{2,1,0:T(8,128)S(1)}, f32[3,8,1024]{2,1,0:T(8,128)S(1)}, u32[]{:S(2)}, u32[]{:S(2)}) collective-permute-start(f32[3,8,1024]{2,1,0:T(8,128)S(1)} %get-tuple-element.50), channel_id=1, source_target_pairs={{0,128},{16,144},{32,160},{48,176},{64,192},{80,208},{96,224},{112... | collective-permute-start | bytes 294920 | tf_op jit(solution)/shard_map/ppermute | solution.py:278
  33.3 6.1 %collective-permute-start.5 = (f32[3,8,1024]{2,1,0:T(8,128)S(1)}, f32[3,8,1024]{2,1,0:T(8,128)S(1)}, u32[]{:S(2)}, u32[]{:S(2)}) collective-permute-start(f32[3,8,1024]{2,1,0:T(8,128)S(1)} %get-tuple-element.51), channel_id=1, source_target_pairs={{0,64},{16,80},{32,96},{48,112},{64,0},{80,16},{96,32},{112,48},{1... | collective-permute-start | bytes 294920 | tf_op jit(solution)/shard_map/ppermute | solution.py:278
  35.8 5.8 %collective-permute-start.6 = (f32[3,8,1024]{2,1,0:T(8,128)S(1)}, f32[3,8,1024]{2,1,0:T(8,128)S(1)}, u32[]{:S(2)}, u32[]{:S(2)}) collective-permute-start(f32[3,8,1024]{2,1,0:T(8,128)S(1)} %get-tuple-element.52), channel_id=1, source_target_pairs={{0,192},{16,208},{32,224},{48,240},{64,128},{80,144},{96,160},{112... | collective-permute-start | bytes 294920 | tf_op jit(solution)/shard_map/ppermute | solution.py:278
  41.7 8.5 %collective-permute-start.16 = (f32[6,8,1024]{2,1,0:T(8,128)S(1)}, f32[6,8,1024]{2,1,0:T(8,128)S(1)}, u32[]{:S(2)}, u32[]{:S(2)}) collective-permute-start(f32[6,8,1024]{2,1,0:T(8,128)S(1)} %shard_map.98), channel_id=1, source_target_pairs={{0,6},{1,31},{2,44},{3,55},{4,64},{5,83},{6,96},{7,123},{8,142},{9... | collective-permute-start | bytes 589832 | tf_op jit(solution)/shard_map/ppermute | solution.py:301
  51.3 18.6 %all-to-all-start = ((f32[16,8,128]{2,1,0:T(8,128)}), f32[16,8,128]{2,1,0:T(8,128)S(1)}, u32[]{:S(2)}, u32[]{:S(2)}) async-start(f32[16,8,128]{2,1,0:T(8,128)} %get-tuple-element.69), calls=%async_computation | async-start | bytes 131072 | tf_op jit(solution)/shard_map/all_to_all | solution.py:317
  71.1 11.1 %all-to-all-start.1 = ((f32[16,8,128]{2,1,0:T(8,128)}), f32[16,8,128]{2,1,0:T(8,128)S(1)}, u32[]{:S(2)}, u32[]{:S(2)}) async-start(f32[16,8,128]{2,1,0:T(8,128)} %get-tuple-element.72), calls=%async_computation.1 | async-start | bytes 131072 | tf_op jit(solution)/shard_map/all_to_all | solution.py:317
